TPU v7x, 128 devices: a whole 4x4x4 slice. The times are simulated.
128 devices in a mesh: data: 1, pair: 128 (over z, y, x, core).
Axes of the slice: x: 4, y: 4, z: 4, core: 2. Of those that a mesh axis runs over, the one named last changes fastest.
Arguments:
- x_enc: bfloat16 [2048, 256, 512], P(('data', 'pair'))
- enc_len: int32 [2048], P(('data', 'pair'))
- y_dec: bfloat16 [2048, 32, 512], P(('data', 'pair'))
- enc_wq: bfloat16 [2, 512, 512], replicated
- enc_wk: bfloat16 [2, 512, 512], replicated
- enc_wv: bfloat16 [2, 512, 512], replicated
- enc_wo: bfloat16 [2, 8, 64, 512], replicated
- enc_w1: bfloat16 [2, 512, 2048], replicated
- enc_w2: bfloat16 [2, 2048, 512], replicated
- dec_wq: bfloat16 [2, 512, 512], replicated
- dec_wk: bfloat16 [2, 512, 512], replicated
- dec_wv: bfloat16 [2, 512, 512], replicated
- dec_wo: bfloat16 [2, 8, 64, 512], replicated
- crs_wq: bfloat16 [2, 512, 512], replicated
- crs_wk: bfloat16 [2, 512, 512], replicated
- crs_wv: bfloat16 [2, 512, 512], replicated
- crs_wo: bfloat16 [2, 8, 64, 512], replicated
- dec_w1: bfloat16 [2, 512, 2048], replicated
- dec_w2: bfloat16 [2, 2048, 512], replicated
Outputs:
- output: bfloat16 [2048, 32, 512], P(('data', 'pair'))
All inputs are finite; a program needn't handle non-finite values.
Results may differ from a plain program's by a relative error of at most 0.0110627.
Values are sent between devices in bfloat16 or wider.
A program may use at most 1 GiB of HBM per device.

v0:
```python
import functools

import jax
import jax.numpy as jnp
from jax import lax
from jax.experimental import pallas as pl
from jax.experimental.pallas import tpu as pltpu
from jax.sharding import PartitionSpec as P

BF = jnp.bfloat16
F32 = jnp.float32
BLK = 256
GRAN = 16
ROWS = 4
GROUP = 2
LAG = 5
XLAG = 3
VMEM_BYTES = 67043328
LIMIT = 1e20
HD = 64
LOG2E = 1.4426950408889634
NEG = -1e30


def dot(a, b):
    return jnp.dot(a, b, preferred_element_type=F32)


def dot_t(a, b):
    return lax.dot_general(a, b, (((1,), (1,)), ((), ())), preferred_element_type=F32)


def norm(x):
    xw = x.astype(F32)
    return (xw * lax.rsqrt(jnp.mean(xw * xw, axis=-1, keepdims=True) + 1e-6)).astype(BF)


def gelu(x):
    inner = x * (0.7978845608028654 + 0.035677408136300125 * (x * x))
    half = 0.5 * x
    return half + half * jnp.tanh(inner)


def ffn(h1s, w1_ref, w2_ref, layer, u_ref):
    hns = [norm(h1) for h1 in h1s]
    ff = w1_ref.shape[2]
    for i, hn in enumerate(hns):
        for c in range(0, ff, 512):
            u_ref[i, :, c:c + 512] = gelu(dot(hn, w1_ref[layer, :, c:c + 512])).astype(BF)
    return [(h1.astype(F32) + dot(u_ref[i], w2_ref[layer])).astype(BF) for i, h1 in enumerate(h1s)]


def score(keys, queries, h):
    pair = slice(128 * (h // 2), 128 * (h // 2) + 128)
    lane = lax.broadcasted_iota(jnp.int32, (queries.shape[0], 2 * HD), 1)
    mine = (lane < HD) if h % 2 == 0 else (lane >= HD)
    return dot_t(keys[:, pair], jnp.where(mine, queries[:, pair], jnp.zeros((), BF)))


def weigh(s, mask=None):
    if mask is not None:
        s = jnp.where(mask, s, NEG)
    return jnp.exp2((s - jnp.max(s, axis=0, keepdims=True)) * LOG2E).astype(BF)


def head_attention(jobs, lag=LAG, shift=True):
    steps = [(job, h, j) for j, job in enumerate(jobs) for h in range(job[0].shape[1] // HD)]
    scores = {}
    reach = [None] * len(jobs)
    for i in range(len(steps) + lag):
        if i < len(steps):
            (keys, queries, _, _, _), h, _ = steps[i]
            scores[i] = score(keys, queries, h)
        if i >= lag:
            (keys, queries, vtx_ref, ctx_ref, mask), h, j = steps[i - lag]
            s = scores.pop(i - lag)
            e = weigh(s, mask) if shift else jnp.exp2(s * LOG2E).astype(BF)
            o = dot(vtx_ref[h, :, :keys.shape[0]], e)
            inverse = 1.0 / o[HD:HD + 1]
            ctx_ref[h * HD:(h + 1) * HD, :queries.shape[0]] = (o[:HD] * inverse).astype(BF)
            if not shift:
                far = jnp.maximum(jnp.max(jnp.abs(o[:HD + 8]), axis=0, keepdims=True), inverse)
                reach[j] = far if reach[j] is None else jnp.maximum(reach[j], far)
    return reach


def store_values(v, vtx_ref, lk):
    vt = v.T
    for h in range(v.shape[1] // HD):
        vtx_ref[h, :HD, :lk] = vt[h * HD:(h + 1) * HD]


def place_rows(len_ref, rows, start_ref, order_ref):
    lens = [len_ref[r] for r in range(rows)]
    ranks = [jnp.int32(0)] * rows
    for r in range(rows):
        for t in range(r):
            later = (lens[t] <= lens[r]).astype(jnp.int32)
            ranks[r] = ranks[r] + later
            ranks[t] = ranks[t] + 1 - later
    for r in range(rows):
        order_ref[ranks[r]] = r
    at = jnp.int32(0)
    for i in range(rows):
        r = order_ref[i]
        start_ref[r] = at
        at = at + (len_ref[r] + (GRAN - 1)) // GRAN * GRAN
    return at


def block_at(b):
    return pl.ds(pl.multiple_of(b * BLK, BLK), BLK)


def over_blocks(blocks, fn):
    def group(g, carry):
        fn([g * GROUP + i for i in range(GROUP)])
        return carry
    lax.fori_loop(0, blocks // GROUP, group, 0)

    @pl.when(blocks % GROUP != 0)
    def _():
        fn([blocks - 1])


def project(bs, hidden, buf, wq, wk, wv):
    hns = [norm(hid) for hid in hidden]
    for b, hn in zip(bs, hns):
        at = block_at(b)
        buf[0, at] = dot(hn, wq[...]).astype(BF) * BF(HD ** -0.5)
        buf[1, at] = dot(hn, wk[...]).astype(BF)
        buf[2, at] = dot(hn, wv[...]).astype(BF)


def row_attention(len_ref, start_ref, order_ref, buf, vtx_ref, ctx_ref, ok_ref):
    rows = len_ref.shape[0]
    seq = vtx_ref.shape[3]

    def attention(i, count, lq, lk, shift):
        jobs, dests = [], []
        for slot in range(count):
            r = order_ref[i * count + slot]
            begin = pl.multiple_of(start_ref[r], GRAN)
            length = len_ref[r]
            at_k, at_q = pl.ds(begin, lk), pl.ds(begin, lq)
            vtx, ctx = vtx_ref.at[slot], ctx_ref.at[slot]
            inside = lax.broadcasted_iota(jnp.int32, (lk, 1), 0) < length
            keys = jnp.where(inside, buf[1, at_k], buf[1, pl.ds(begin, GRAN)][:1])
            store_values(jnp.where(inside, buf[2, at_k], jnp.zeros((), BF)), vtx, lk)
            weight = (lax.broadcasted_iota(jnp.int32, (GRAN, lk), 1) < length).astype(F32).astype(BF)
            for h in range(vtx_ref.shape[1]):
                vtx[h, HD:HD + GRAN, :lk] = weight
            jobs.append((keys, buf[0, at_q], vtx, ctx, None))
            dests.append((at_q, ctx, length))
        reach = head_attention(jobs, shift=shift)
        for (at_q, ctx, length), far in zip(dests, reach):
            buf[3, at_q] = ctx[:, :lq].T
            if far is not None:
                inside = lax.broadcasted_iota(jnp.int32, (1, lq), 1) < length
                ok = jnp.where((far < LIMIT) | (~inside), 1.0, 0.0)
                ok_ref[:1, :lq] = jnp.minimum(ok_ref[:1, :lq], ok)

    ok_ref[...] = jnp.ones(ok_ref.shape, F32)

    def attend_rows(i, carry):
        longest = len_ref[order_ref[i * ROWS + ROWS - 1]]
        for low, high in ((0, 128), (128, 192), (192, 256)):
            @pl.when((longest > low) & (longest <= high))
            def _(high=high):
                attention(i, ROWS, (high + 127) // 128 * 128, high, False)
        return carry
    lax.fori_loop(0, rows // ROWS, attend_rows, 0)

    @pl.when(jnp.min(ok_ref[...]) < 0.5)
    def _():
        def attend_row(i, carry):
            attention(i, 1, seq, seq, True)
            return carry
        lax.fori_loop(0, rows, attend_row, 0)


def front_kernel(rows, seq, len_ref, x_hbm, wq_h, wk_h, wv_h, h_hbm, c_hbm,
                 h_ref, buf, vtx_ref, ctx_ref, wq, wk, wv, ok_ref, start_ref, order_ref, x_sem, w_sem, o_sem):
    def x_copy(r):
        return pltpu.make_async_copy(x_hbm.at[r], buf.at[3, pl.ds(pl.multiple_of(r * seq, seq), seq)], x_sem.at[r])

    for r in range(rows):
        x_copy(r).start()
    w_copies = [pltpu.make_async_copy(src.at[0], dst, w_sem.at[i]) for i, (src, dst) in enumerate([(wq_h, wq), (wk_h, wk), (wv_h, wv)])]
    for copy in w_copies:
        copy.start()
    blocks = (place_rows(len_ref, rows, start_ref, order_ref) + (BLK - 1)) // BLK

    def pack(i, carry):
        r = order_ref[i]
        x_copy(r).wait()
        h_ref[pl.ds(pl.multiple_of(start_ref[r], GRAN), seq)] = buf[3, pl.ds(pl.multiple_of(r * seq, seq), seq)]
        return carry
    lax.fori_loop(0, rows, pack, 0)
    for copy in w_copies:
        copy.wait()

    def h_copy(b):
        return pltpu.make_async_copy(h_ref.at[block_at(b)], h_hbm.at[block_at(b)], o_sem.at[0, b])

    def c_copy(b):
        return pltpu.make_async_copy(buf.at[3, block_at(b)], c_hbm.at[block_at(b)], o_sem.at[1, b])

    def first(bs):
        for b in bs:
            h_copy(b).start()
        project(bs, [h_ref[block_at(b)] for b in bs], buf, wq, wk, wv)
    over_blocks(blocks, first)
    row_attention(len_ref, start_ref, order_ref, buf, vtx_ref, ctx_ref, ok_ref)

    def send(b, carry):
        c_copy(b).start()
        return carry
    lax.fori_loop(0, blocks, send, 0)

    def finish(b, carry):
        h_copy(b).wait()
        c_copy(b).wait()
        return carry
    lax.fori_loop(0, blocks, finish, 0)


def front(x_enc, enc_len, wq, wk, wv):
    rows, seq, d = x_enc.shape
    heads = d // HD
    tokens = rows * seq + seq
    any_spec = pl.BlockSpec(memory_space=pl.ANY)
    out = jax.ShapeDtypeStruct((tokens, d), BF)
    return pl.pallas_call(
        functools.partial(front_kernel, rows, seq),
        out_shape=(out, out),
        in_specs=[pl.BlockSpec(memory_space=pltpu.SMEM)] + [any_spec] * 4,
        out_specs=(any_spec, any_spec),
        scratch_shapes=[pltpu.VMEM((tokens, d), BF), pltpu.VMEM((4, tokens, d), BF),
                        pltpu.VMEM((ROWS, heads, HD + GRAN, seq), BF), pltpu.VMEM((ROWS, d, seq), BF)]
        + [pltpu.VMEM(w.shape[1:], BF) for w in (wq, wk, wv)]
        + [pltpu.VMEM((8, seq), F32), pltpu.SMEM((rows,), jnp.int32), pltpu.SMEM((rows,), jnp.int32),
           pltpu.SemaphoreType.DMA((rows,)), pltpu.SemaphoreType.DMA((3,)), pltpu.SemaphoreType.DMA((2, tokens // BLK))],
        compiler_params=pltpu.CompilerParams(vmem_limit_bytes=50 * 1024 * 1024),
        cost_estimate=pl.CostEstimate(flops=30_000_000_000, bytes_accessed=15_000_000, transcendentals=0),
        name="front",
    )(enc_len, x_enc, wq, wk, wv)


def back_kernel(rows, seq, len_ref, h_hbm, c_hbm, y_hbm, wq_h, wk_h, wv_h, wo_h, w1_h, w2_h, cwk_h, cwv_h,
                dq_h, dk_h, dv_h, do_h, xq_h, xo_h, d1_h, d2_h, out_hbm,
                h_ref, buf, u_ref, vtx_ref, ctx_ref, z_ref, cq_ref, cc_ref,
                wq, wk, wv, wo, w1, w2, cwk, cwv, dq, dk, dv, do, xq, xo, d1, d2,
                ok_ref, start_ref, order_ref, t_sem, e_sem, d_sem, y_sem):
    layers = wo_h.shape[0]
    blocks = (place_rows(len_ref, rows, start_ref, order_ref) + (BLK - 1)) // BLK

    def token_copies(b):
        at = block_at(b)
        return (pltpu.make_async_copy(h_hbm.at[at], h_ref.at[at], t_sem.at[0, b]),
                pltpu.make_async_copy(c_hbm.at[at], buf.at[3, at], t_sem.at[1, b]))

    def start_tokens(b, carry):
        for copy in token_copies(b):
            copy.start()
        return carry

    enc = [(wo_h, wo), (w1_h, w1), (w2_h, w2), (cwk_h, cwk), (cwv_h, cwv)]
    qkv = [(wq_h, wq), (wk_h, wk), (wv_h, wv)]
    dec_pairs = [(dq_h, dq), (dk_h, dk), (dv_h, dv), (do_h, do), (xq_h, xq), (xo_h, xo), (d1_h, d1), (d2_h, d2)]

    def enc_copy(i, layer):
        return pltpu.make_async_copy(enc[i][0].at[layer], enc[i][1].at[layer], e_sem.at[i, layer])

    def qkv_copy(i, layer):
        return pltpu.make_async_copy(qkv[i][0].at[layer], qkv[i][1].at[layer - 1], e_sem.at[5 + i, layer])

    def dec_copy(i, layer):
        return pltpu.make_async_copy(dec_pairs[i][0].at[layer], dec_pairs[i][1].at[layer], d_sem.at[i, layer])

    enc_copy(0, 0).start()
    lax.fori_loop(0, jnp.minimum(blocks, GROUP), start_tokens, 0)
    enc_copy(1, 0).start()
    enc_copy(2, 0).start()
    for layer in range(1, layers):
        for i in range(3):
            qkv_copy(i, layer).start()
    lax.fori_loop(GROUP, blocks, start_tokens, 0)
    for layer in range(1, layers):
        for i in range(3):
            enc_copy(i, layer).start()
    for layer in range(layers):
        for i in range(3, 5):
            enc_copy(i, layer).start()
    y_copy = pltpu.make_async_copy(y_hbm, z_ref, y_sem)
    y_copy.start()
    for layer in range(layers):
        for i in range(8):
            dec_copy(i, layer).start()

    for layer in range(layers):
        if layer > 0:
            row_attention(len_ref, start_ref, order_ref, buf, vtx_ref, ctx_ref, ok_ref)
        for i in range(3):
            enc_copy(i, layer).wait()
        if layer + 1 < layers:
            for i in range(3):
                qkv_copy(i, layer + 1).wait()
        else:
            for other in range(layers):
                for i in range(3, 5):
                    enc_copy(i, other).wait()

        def dense(bs, layer=layer):
            if layer == 0:
                for b in bs:
                    for copy in token_copies(b):
                        copy.wait()
            h1s = [(h_ref[block_at(b)].astype(F32) + dot(buf[3, block_at(b)], wo[layer])).astype(BF) for b in bs]
            h2s = ffn(h1s, w1, w2, layer, u_ref)
            if layer + 1 < layers:
                for b, h2 in zip(bs, h2s):
                    h_ref[block_at(b)] = h2
                project(bs, h2s, buf, wq.at[layer], wk.at[layer], wv.at[layer])
            else:
                outs = [norm(h2) for h2 in h2s]
                for b, out in zip(bs, outs):
                    for other in range(layers):
                        buf[2 * other, block_at(b)] = dot(out, cwk[other]).astype(BF)
                        buf[2 * other + 1, block_at(b)] = dot(out, cwv[other]).astype(BF)
        over_blocks(blocks, dense)

    dec = y_hbm.shape[0] // rows
    m = BLK
    per_block = m // dec
    heads = ctx_ref.shape[1] // HD
    bs = range(rows // per_block)
    y_copy.wait()
    ki = lax.broadcasted_iota(jnp.int32, (m, m), 0)
    qi = lax.broadcasted_iota(jnp.int32, (m, m), 1)
    causal = (ki <= qi) & (ki // dec == qi // dec)
    for b in bs:
        vtx_ref[b, :, HD:HD + GRAN, :] = jnp.ones((heads, GRAN, m), BF)
    lane = lax.broadcasted_iota(jnp.int32, (dec, heads * HD), 1)

    def layer_step(layer, carry):
        for i in range(8):
            dec_copy(i, layer).wait()
        z = [z_ref[b * m:(b + 1) * m] for b in bs]
        zn = [norm(x) for x in z]
        jobs = []
        for b in bs:
            q = dot(zn[b], dq[layer]).astype(BF) * BF(HD ** -0.5)
            k = dot(zn[b], dk[layer]).astype(BF)
            store_values(dot(zn[b], dv[layer]).astype(BF), vtx_ref.at[b], m)
            jobs.append((k, q, vtx_ref.at[b], ctx_ref.at[b], causal))
        head_attention(jobs)
        z1 = [(z[b].astype(F32) + dot(ctx_ref[b].T, do[layer])).astype(BF) for b in bs]
        z1n = [norm(x) for x in z1]
        for b in bs:
            cq_ref[b * m:(b + 1) * m] = dot(z1n[b], xq[layer]).astype(BF) * BF(HD ** -0.5)

        def scores(row):
            qr = cq_ref[row * dec:(row + 1) * dec]
            qs = jnp.concatenate([jnp.where(lane // HD == h, qr, jnp.zeros((), BF)) for h in range(heads)], axis=0)
            return dot_t(qs, buf[2 * layer, pl.ds(pl.multiple_of(start_ref[row], GRAN), seq)])

        def context(row, s):
            length = len_ref[row]
            s = jnp.where(lax.broadcasted_iota(jnp.int32, (1, seq), 1) < length, s, NEG)
            top = jnp.max(s, axis=1, keepdims=True)
            e = jnp.exp2((s - top) * LOG2E)
            p = (e * (1.0 / jnp.sum(e, axis=1, keepdims=True))).astype(BF)
            vals = buf[2 * layer + 1, pl.ds(pl.multiple_of(start_ref[row], GRAN), seq)]
            vals = jnp.where(lax.broadcasted_iota(jnp.int32, (seq, 1), 0) < length, vals, jnp.zeros((), BF))
            o = dot(p, vals)
            first = lax.broadcasted_iota(jnp.int32, (dec, 2 * HD), 1) < HD
            for j in range(heads // 2):
                cols = slice(128 * j, 128 * j + 128)
                cc_ref[row * dec:(row + 1) * dec, cols] = jnp.where(
                    first, o[2 * j * dec:(2 * j + 1) * dec, cols], o[(2 * j + 1) * dec:(2 * j + 2) * dec, cols]).astype(BF)

        pending = {}
        for i in range(rows + XLAG):
            if i < rows:
                pending[i] = scores(i)
            if i >= XLAG:
                context(i - XLAG, pending.pop(i - XLAG))
        z2 = [(z1[b].astype(F32) + dot(cc_ref[b * m:(b + 1) * m], xo[layer])).astype(BF) for b in bs]
        for b, x in zip(bs, ffn(z2, d1, d2, layer, u_ref)):
            z_ref[b * m:(b + 1) * m] = x
        return carry
    lax.fori_loop(0, layers, layer_step, 0)

    out_copy = pltpu.make_async_copy(z_ref, out_hbm, y_sem)
    out_copy.start()
    out_copy.wait()


def back(enc_len, h, c, y, seq, enc_weights, dec_weights):
    rows, dec, d = y.shape
    wq, wk, wv, wo, w1, w2, cwk, cwv = enc_weights
    layers, ff = w1.shape[0], w1.shape[2]
    heads = d // HD
    tokens = h.shape[0]
    any_spec = pl.BlockSpec(memory_space=pl.ANY)
    out = pl.pallas_call(
        functools.partial(back_kernel, rows, seq),
        out_shape=jax.ShapeDtypeStruct((rows * dec, d), BF),
        in_specs=[pl.BlockSpec(memory_space=pltpu.SMEM)] + [any_spec] * 19,
        out_specs=any_spec,
        scratch_shapes=[pltpu.VMEM((tokens, d), BF), pltpu.VMEM((4, tokens, d), BF), pltpu.VMEM((GROUP, BLK, ff), BF),
                        pltpu.VMEM((ROWS, heads, HD + GRAN, seq), BF), pltpu.VMEM((ROWS, d, seq), BF),
                        pltpu.VMEM((rows * dec, d), BF), pltpu.VMEM((rows * dec, d), BF), pltpu.VMEM((rows * dec, d), BF)]
        + [pltpu.VMEM((layers - 1,) + w.shape[1:], BF) for w in (wq, wk, wv)]
        + [pltpu.VMEM(w.shape, BF) for w in (wo, w1, w2, cwk, cwv) + dec_weights]
        + [pltpu.VMEM((8, seq), F32), pltpu.SMEM((rows,), jnp.int32), pltpu.SMEM((rows,), jnp.int32),
           pltpu.SemaphoreType.DMA((2, tokens // BLK)), pltpu.SemaphoreType.DMA((8, layers)), pltpu.SemaphoreType.DMA((8, layers)), pltpu.SemaphoreType.DMA],
        compiler_params=pltpu.CompilerParams(vmem_limit_bytes=VMEM_BYTES),
        cost_estimate=pl.CostEstimate(flops=60_000_000_000, bytes_accessed=40_000_000, transcendentals=0),
        name="back",
    )(enc_len, h, c, y.reshape(rows * dec, d), *enc_weights, *dec_weights)
    return out.reshape(rows, dec, d)


def solution(mesh):
    pair_size = mesh.shape["pair"]
    to_partner = [(source, (source + pair_size // 2) % pair_size) for source in range(pair_size)]
    row_spec = P(("data", "pair"))
    full_spec = P()

    def per_device(x_enc, enc_len, y_dec, enc_wq, enc_wk, enc_wv, enc_wo, enc_w1, enc_w2, dec_wq, dec_wk, dec_wv, dec_wo, crs_wq, crs_wk, crs_wv, crs_wo, dec_w1, dec_w2):
        d = x_enc.shape[2]
        flat = lambda w: w.reshape(w.shape[0], w.shape[1] * w.shape[2], d)
        y_here = lax.ppermute(y_dec, "pair", to_partner)
        h, c = front(x_enc, enc_len, enc_wq, enc_wk, enc_wv)
        out_here = back(enc_len, h, c, y_here, x_enc.shape[1],
                        (enc_wq, enc_wk, enc_wv, flat(enc_wo), enc_w1, enc_w2, crs_wk, crs_wv),
                        (dec_wq, dec_wk, dec_wv, flat(dec_wo), crs_wq, flat(crs_wo), dec_w1, dec_w2))
        return lax.ppermute(out_here, "pair", to_partner)

    return jax.shard_map(per_device, mesh=mesh, in_specs=(row_spec, row_spec, row_spec) + (full_spec,) * 16, out_specs=row_spec, check_vma=False)
```

profile of v0, /device:TPU:39, one launch (start us, length us, event | category | flops | bytes accessed | tf_op | source)
XLA Modules:
  0.0 126.5 jit_solution(15660702055647186208)
XLA Ops:
  0.0 2.7 %collective-permute-start = (bf16[16,32,512]{2,1,0:T(8,128)(2,1)}, bf16[16,32,512]{2,1,0:T(8,128)(2,1)}, u32[]{:S(2)}, u32[]{:S(2)}) collective-permute-start(bf16[16,32,512]{2,1,0:T(8,128)(2,1)} %param.21), channel_id=1, source_target_pairs={{0,64},{1,65},{2,66},{3,67},{4,68},{5,69},{6,70},{7,71},{8,72},{9,... | collective-permute-start | bytes 1572872 | tf_op jit(solution)/shard_map/ppermute | solution.py:435
  2.7 0.0 copy-start
  2.7 1.2 copy-done
  3.9 0.0 copy-start.1
  3.9 1.2 copy-done.1
  5.1 0.0 copy-start.2
  5.2 1.2 copy-done.2
  6.4 0.0 copy-start.3
  6.4 0.7 copy-done.3
  7.0 20.6 %front.1 = (bf16[4352,512]{1,0:T(8,128)(2,1)}, bf16[4352,512]{1,0:T(8,128)(2,1)}) custom-call(s32[16]{0:T(128)S(1)} %copy-done.3, bf16[16,256,512]{2,1,0:T(8,128)(2,1)} %x_hbm.1, bf16[2,512,512]{2,1,0:T(8,128)(2,1)S(1)} %copy-done, bf16[2,512,512]{2,1,0:T(8,128)(2,1)S(1)} %copy-done.1, bf16[2,512,512]{2,1,0:T(8,128)(2,1)S(1)} %copy-done.2), custom_call_target="tpu_custom_call" | custom-call | flops 30000001024 | bytes 15000000 | tf_op jit(solution)/shard_map/front/pallas_call | solution.py:234
  27.7 0.0 collective-permute-done
  27.7 87.5 %back.1 = bf16[512,512]{1,0:T(8,128)(2,1)} custom-call(s32[16]{0:T(128)} %len_ref.3, bf16[4352,512]{1,0:T(8,128)(2,1)} %get-tuple-element.7.h_hbm, bf16[4352,512]{1,0:T(8,128)(2,1)} %get-tuple-element.8.c_hbm, bf16[512,512]{1,0:T(8,128)(2,1)} %bitcast.y_hbm, bf16[2,512,512]{2,1,0:T(8,128)(2,1)} %wq_h.3, bf16[2,512,512]{2,1,0:T(8,128)(2,1)} %wk_h.3, ...), custom_call_target="tpu_custom_call" | custom-call | flops 60000002048 | bytes 40000000 | tf_op jit(solution)/shard_map/back/pallas_call | solution.py:407
  115.2 0.1 collective-permute-start.1
  115.3 10.4 %collective-permute-done.1 = bf16[16,32,512]{2,1,0:T(8,128)(2,1)S(1)} collective-permute-done((bf16[16,32,512]{2,1,0:T(8,128)(2,1)}, bf16[16,32,512]{2,1,0:T(8,128)(2,1)S(1)}, u32[]{:S(2)}, u32[]{:S(2)}) %collective-permute-start.1) | collective-permute-done | bytes 524320 | tf_op jit(solution)/shard_map/ppermute | solution.py:440
  125.7 0.8 copy.21
Async XLA Ops:
  0.0 27.7 %collective-permute-start = (bf16[16,32,512]{2,1,0:T(8,128)(2,1)}, bf16[16,32,512]{2,1,0:T(8,128)(2,1)}, u32[]{:S(2)}, u32[]{:S(2)}) collective-permute-start(bf16[16,32,512]{2,1,0:T(8,128)(2,1)} %param.21), channel_id=1, source_target_pairs={{0,64},{1,65},{2,66},{3,67},{4,68},{5,69},{6,70},{7,71},{8,72},{9,... | collective-permute-start | bytes 1572872 | tf_op jit(solution)/shard_map/ppermute | solution.py:435
  2.7 1.2 copy-start
  3.9 1.2 copy-start.1
  5.1 1.2 copy-start.2
  6.4 0.7 copy-start.3
  115.2 10.5 %collective-permute-start.1 = (bf16[16,32,512]{2,1,0:T(8,128)(2,1)}, bf16[16,32,512]{2,1,0:T(8,128)(2,1)S(1)}, u32[]{:S(2)}, u32[]{:S(2)}) collective-permute-start(bf16[16,32,512]{2,1,0:T(8,128)(2,1)} %bitcast.8), channel_id=1, source_target_pairs={{0,64},{1,65},{2,66},{3,67},{4,68},{5,69},{6,70},{7,71},{8,72},{9,... | collective-permute-start | bytes 1572872 | tf_op jit(solution)/shard_map/ppermute | solution.py:440
where the time goes:
time: 129 us; the launch traced here: 127 us
  Pallas kernels  108 us (84%)
  waiting for transfers between devices  10.4 us (8%)
  local copies, waits for them, and re-layouts  5.12 us (4%)
  starting transfers between devices  2.78 us (2%)
    pallas_call x1, Pallas kernels, back(): pl.pallas_call(functools.partial(back_kernel, rows, seq), out_shape=jax.S...  87.5 us
    pallas_call x1, Pallas kernels, front(): pl.pallas_call(functools.partial(front_kernel, rows, seq), out_shape=(out...  20.6 us
    ppermute x1, waiting for transfers between devices, per_device(): return lax.ppermute(out_here, 'pair', to_partner)  10.4 us
    unnamed x9, local copies, waits for them, and re-layouts  5.12 us
    ppermute x1, starting transfers between devices, per_device(): y_here = lax.ppermute(y_dec, 'pair', to_partner)  2.7 us
  transfers between devices with their start and end apart: 2, of which 1 were waited for; matrix products, arithmetic and copies ran while one was open for 0% of the time, Pallas kernels for 16%

commit v1 on v0

--- a/solution.py
+++ b/solution.py
@@ -30,31 +30,31 @@
     return lax.dot_general(a, b, (((1,), (1,)), ((), ())), preferred_element_type=F32)
 
 
-def norm(x):
+def norm(x, scale=1.0):
     xw = x.astype(F32)
-    return (xw * lax.rsqrt(jnp.mean(xw * xw, axis=-1, keepdims=True) + 1e-6)).astype(BF)
-
-
-def gelu(x):
-    inner = x * (0.7978845608028654 + 0.035677408136300125 * (x * x))
-    half = 0.5 * x
+    inv_rms = lax.rsqrt(jnp.mean(xw * xw, axis=-1, keepdims=True) + 1e-6)
+    return (xw * (inv_rms * scale)).astype(BF)
+
+
+def gelu_of_half(half):
+    inner = half * (2 * 0.7978845608028654 + 8 * 0.035677408136300125 * (half * half))
     return half + half * jnp.tanh(inner)
 
 
 def ffn(h1s, w1_ref, w2_ref, layer, u_ref):
-    hns = [norm(h1) for h1 in h1s]
+    hns = [norm(h1, 0.5) for h1 in h1s]
     ff = w1_ref.shape[2]
     for i, hn in enumerate(hns):
         for c in range(0, ff, 512):
-            u_ref[i, :, c:c + 512] = gelu(dot(hn, w1_ref[layer, :, c:c + 512])).astype(BF)
+            u_ref[i, :, c:c + 512] = gelu_of_half(dot(hn, w1_ref[layer, :, c:c + 512])).astype(BF)
     return [(h1.astype(F32) + dot(u_ref[i], w2_ref[layer])).astype(BF) for i, h1 in enumerate(h1s)]
 
 
 def score(keys, queries, h):
     pair = slice(128 * (h // 2), 128 * (h // 2) + 128)
-    lane = lax.broadcasted_iota(jnp.int32, (queries.shape[0], 2 * HD), 1)
+    lane = lax.broadcasted_iota(jnp.int32, (keys.shape[0], 2 * HD), 1)
     mine = (lane < HD) if h % 2 == 0 else (lane >= HD)
-    return dot_t(keys[:, pair], jnp.where(mine, queries[:, pair], jnp.zeros((), BF)))
+    return dot_t(jnp.where(mine, keys[:, pair], jnp.zeros((), BF)), queries[:, pair])
 
 
 def weigh(s, mask=None):
@@ -241,7 +241,7 @@
         + [pltpu.VMEM(w.shape[1:], BF) for w in (wq, wk, wv)]
         + [pltpu.VMEM((8, seq), F32), pltpu.SMEM((rows,), jnp.int32), pltpu.SMEM((rows,), jnp.int32),
            pltpu.SemaphoreType.DMA((rows,)), pltpu.SemaphoreType.DMA((3,)), pltpu.SemaphoreType.DMA((2, tokens // BLK))],
-        compiler_params=pltpu.CompilerParams(vmem_limit_bytes=50 * 1024 * 1024),
+        compiler_params=pltpu.CompilerParams(vmem_limit_bytes=VMEM_BYTES),
         cost_estimate=pl.CostEstimate(flops=30_000_000_000, bytes_accessed=15_000_000, transcendentals=0),
         name="front",
     )(enc_len, x_enc, wq, wk, wv)
@@ -341,7 +341,6 @@
     causal = (ki <= qi) & (ki // dec == qi // dec)
     for b in bs:
         vtx_ref[b, :, HD:HD + GRAN, :] = jnp.ones((heads, GRAN, m), BF)
-    lane = lax.broadcasted_iota(jnp.int32, (dec, heads * HD), 1)
 
     def layer_step(layer, carry):
         for i in range(8):
@@ -362,8 +361,15 @@
 
         def scores(row):
             qr = cq_ref[row * dec:(row + 1) * dec]
-            qs = jnp.concatenate([jnp.where(lane // HD == h, qr, jnp.zeros((), BF)) for h in range(heads)], axis=0)
-            return dot_t(qs, buf[2 * layer, pl.ds(pl.multiple_of(start_ref[row], GRAN), seq)])
+            keys = buf[2 * layer, pl.ds(pl.multiple_of(start_ref[row], GRAN), seq)]
+            first = lax.broadcasted_iota(jnp.int32, (dec, 2 * HD), 1) < HD
+            parts = []
+            for j in range(heads // 2):
+                cols = slice(128 * j, 128 * j + 128)
+                zero = jnp.zeros((), BF)
+                qs = jnp.concatenate([jnp.where(first, qr[:, cols], zero), jnp.where(first, zero, qr[:, cols])], axis=0)
+                parts.append(dot_t(qs, keys[:, cols]))
+            return jnp.concatenate(parts, axis=0)
 
         def context(row, s):
             length = len_ref[row]

time: 129 us -> 123 us (0.953)
  the two profiles are of different devices: /device:TPU:39 before, /device:TPU:15 now
where the time goes in v1:
time: 123 us
  Pallas kernels  107 us (87%)
  waiting for transfers between devices  11.2 us (9%)
  starting transfers between devices  3.68 us (3%)
    pallas_call x1, Pallas kernels, back(): pl.pallas_call(functools.partial(back_kernel, rows, seq), out_shape=jax.S...  86.1 us
    pallas_call x1, Pallas kernels, front(): pl.pallas_call(functools.partial(front_kernel, rows, seq), out_shape=(out...  20.8 us
    ppermute x1, waiting for transfers between devices, per_device(): return lax.ppermute(out_here, 'pair', to_partner)  11.2 us
    ppermute x1, starting transfers between devices, per_device(): y_here = lax.ppermute(y_dec, 'pair', to_partner)  3.6 us
  transfers between devices with their start and end apart: 2, of which 1 were waited for; matrix products, arithmetic and copies ran while one was open for 0% of the time, Pallas kernels for 17%

profile of v1, /device:TPU:15, one launch (start us, length us, event | category | flops | bytes accessed | tf_op | source)
XLA Modules:
  0.0 122.6 jit_solution(15373339563877040642)
XLA Ops:
  0.0 3.6 %collective-permute-start = (bf16[16,32,512]{2,1,0:T(8,128)(2,1)}, bf16[16,32,512]{2,1,0:T(8,128)(2,1)}, u32[]{:S(2)}, u32[]{:S(2)}) collective-permute-start(bf16[16,32,512]{2,1,0:T(8,128)(2,1)} %param.21), channel_id=1, source_target_pairs={{0,64},{1,65},{2,66},{3,67},{4,68},{5,69},{6,70},{7,71},{8,72},{9,... | collective-permute-start | bytes 1572872 | tf_op jit(solution)/shard_map/ppermute | solution.py:441
  3.6 20.8 %front.1 = (bf16[4352,512]{1,0:T(8,128)(2,1)}, bf16[4352,512]{1,0:T(8,128)(2,1)}) custom-call(s32[16]{0:T(128)} %len_ref.3, bf16[16,256,512]{2,1,0:T(8,128)(2,1)} %x_hbm.1, bf16[2,512,512]{2,1,0:T(8,128)(2,1)} %wq_h.3, bf16[2,512,512]{2,1,0:T(8,128)(2,1)} %wk_h.3, bf16[2,512,512]{2,1,0:T(8,128)(2,1)} %wv_h.3), custom_call_target="tpu_custom_call" | custom-call | flops 30000001024 | bytes 15000000 | tf_op jit(solution)/shard_map/front/pallas_call | solution.py:234
  24.4 0.0 collective-permute-done
  24.4 86.1 %back.1 = bf16[512,512]{1,0:T(8,128)(2,1)} custom-call(s32[16]{0:T(128)} %len_ref.3, bf16[4352,512]{1,0:T(8,128)(2,1)} %get-tuple-element.7.h_hbm, bf16[4352,512]{1,0:T(8,128)(2,1)} %get-tuple-element.8.c_hbm, bf16[512,512]{1,0:T(8,128)(2,1)} %bitcast.y_hbm, bf16[2,512,512]{2,1,0:T(8,128)(2,1)} %wq_h.3, bf16[2,512,512]{2,1,0:T(8,128)(2,1)} %wk_h.3, ...), custom_call_target="tpu_custom_call" | custom-call | flops 60000002048 | bytes 40000000 | tf_op jit(solution)/shard_map/back/pallas_call | solution.py:413
  110.5 0.1 collective-permute-start.1
  110.6 11.2 %collective-permute-done.1 = bf16[16,32,512]{2,1,0:T(8,128)(2,1)S(1)} collective-permute-done((bf16[16,32,512]{2,1,0:T(8,128)(2,1)}, bf16[16,32,512]{2,1,0:T(8,128)(2,1)S(1)}, u32[]{:S(2)}, u32[]{:S(2)}) %collective-permute-start.1) | collective-permute-done | bytes 524320 | tf_op jit(solution)/shard_map/ppermute | solution.py:446
  121.8 0.8 copy.21
Async XLA Ops:
  0.0 24.4 %collective-permute-start = (bf16[16,32,512]{2,1,0:T(8,128)(2,1)}, bf16[16,32,512]{2,1,0:T(8,128)(2,1)}, u32[]{:S(2)}, u32[]{:S(2)}) collective-permute-start(bf16[16,32,512]{2,1,0:T(8,128)(2,1)} %param.21), channel_id=1, source_target_pairs={{0,64},{1,65},{2,66},{3,67},{4,68},{5,69},{6,70},{7,71},{8,72},{9,... | collective-permute-start | bytes 1572872 | tf_op jit(solution)/shard_map/ppermute | solution.py:441
  110.5 11.3 %collective-permute-start.1 = (bf16[16,32,512]{2,1,0:T(8,128)(2,1)}, bf16[16,32,512]{2,1,0:T(8,128)(2,1)S(1)}, u32[]{:S(2)}, u32[]{:S(2)}) collective-permute-start(bf16[16,32,512]{2,1,0:T(8,128)(2,1)} %bitcast.8), channel_id=1, source_target_pairs={{0,64},{1,65},{2,66},{3,67},{4,68},{5,69},{6,70},{7,71},{8,72},{9,... | collective-permute-start | bytes 1572872 | tf_op jit(solution)/shard_map/ppermute | solution.py:446
